TPU v7x, 32 devices: a whole 2x2x4 slice. The times are simulated.
32 devices in a mesh: blk: 8 (over z, x), shard: 4 (over y, core).
Axes of the slice: x: 2, y: 2, z: 4, core: 2. Of those that a mesh axis runs over, the one named last changes fastest.
Arguments:
- tokens: bfloat16 [8192, 2048], P(('blk', 'shard')), may hold values from -6 to 6
- targets: bfloat16 [8192, 2048], P(('blk', 'shard')), may hold values from -6 to 6
- up_weight: bfloat16 [2048, 7168], P(None, 'shard'), may hold values from -0.125 to 0.125
- down_weight: bfloat16 [8, 7168, 2048], P('blk', 'shard'), may hold values from -6 to 6
- mix_numer: int32 [2, 8, 3], replicated, may hold values from 1 to 2, as said below
Outputs:
- drift: bfloat16 [8, 7168, 2048], P('blk', 'shard')
Inputs may be any that keep to these rules, and one draw needn't show every extreme that they name: Each row of mix_numer is (2, 1, 1), (1, 2, 1) or (1, 1, 2).
All inputs are finite; a program needn't handle non-finite values.
Results may differ from a plain program's by a relative error of at most 0.017.
Values may be sent and summed in bfloat16 or wider, within the bound.
No kernel may reach another device: no remote copies, remote signals or barrier semaphores. Data moves between devices by JAX's collectives and lax.ppermute only.
A program may use at most 128 MiB of HBM per device.

v0:
```python
import jax
import jax.numpy as jnp
from jax import lax
from jax.sharding import PartitionSpec as P

FF = 7168
learn_rate = 2.0


def passed_along(x, axis, by):
    devices = lax.axis_size(axis)
    return lax.ppermute(x, axis, [(i, (i + by) % devices) for i in range(devices)])


def combine(center, left, right, weights):
    total = (
        weights[0] * center.astype(jnp.float32)
        + weights[1] * left.astype(jnp.float32)
        + weights[2] * right.astype(jnp.float32)
    )
    return (total / 4.0).astype(jnp.bfloat16)


def numer_of(mix_numer, round_index, worker):
    return lax.dynamic_index_in_dim(mix_numer[round_index], worker, 0, keepdims=False).astype(
        jnp.float32
    )


def body(tokens, targets, up_weight, down_weight, mix_numer):
    weight = down_weight[0]
    out_scale = 1.0 / jnp.sqrt(jnp.float32(FF))
    hidden = jax.nn.silu(
        jnp.dot(
            lax.all_gather(tokens, "shard", axis=0, tiled=True),
            up_weight,
            preferred_element_type=jnp.float32,
        )
    ).astype(jnp.bfloat16)
    rows = hidden
    output = lax.psum_scatter(
        (jnp.dot(rows, weight, preferred_element_type=jnp.float32) * out_scale).astype(
            jnp.bfloat16
        ),
        "shard",
        scatter_dimension=0,
        tiled=True,
    ).astype(jnp.float32)
    resid = (output - targets.astype(jnp.float32)).astype(jnp.bfloat16)
    rows = hidden
    grad = lax.dot_general(
        rows,
        lax.all_gather(resid, "shard", axis=0, tiled=True),
        (((0,), (0,)), ((), ())),
        preferred_element_type=jnp.float32,
    )
    stepped = (weight.astype(jnp.float32) - learn_rate * grad * out_scale).astype(jnp.bfloat16)
    worker = lax.axis_index("blk")
    workers = lax.axis_size("blk")
    near_left = passed_along(stepped, "blk", 1)
    near_right = passed_along(stepped, "blk", -1)
    far_left = passed_along(stepped, "blk", 2)
    far_right = passed_along(stepped, "blk", -2)
    left_worker = (worker - 1) % workers
    right_worker = (worker + 1) % workers
    first_left = combine(near_left, far_left, stepped, numer_of(mix_numer, 0, left_worker))
    first_self = combine(stepped, near_left, near_right, numer_of(mix_numer, 0, worker))
    first_right = combine(near_right, stepped, far_right, numer_of(mix_numer, 0, right_worker))
    mixed = combine(first_self, first_left, first_right, numer_of(mix_numer, 1, worker))
    total = lax.psum(mixed.astype(jnp.float32).astype(jnp.bfloat16), "blk").astype(jnp.float32)
    average = total / jnp.float32(workers)
    return (mixed.astype(jnp.float32) - average).astype(jnp.bfloat16)[None]


def solution(mesh):
    in_specs = (
        P(("blk", "shard"), None),
        P(("blk", "shard"), None),
        P(None, "shard"),
        P("blk", "shard", None),
        P(),
    )
    out_specs = P("blk", "shard", None)
    return jax.shard_map(body, mesh=mesh, in_specs=in_specs, out_specs=out_specs, check_vma=False)
```

profile of v0, /device:TPU:0, one launch (start us, length us, event | category | flops | bytes accessed | tf_op | source)
XLA Modules:
  0.0 932.1 jit_solution(15724398511861249869)
XLA Ops:
  6.5 0.7 all-gather.3.cloned.1.call-update
  7.3 38.8 %all-gather.3.cloned.1.call-done = bf16[1024,2048]{1,0:T(8,128)(2,1)} async-done(((bf16[256,2048]{1,0:T(8,128)(2,1)}), bf16[1024,2048]{1,0:T(8,128)(2,1)}) %all-gather.3.cloned.1.call-update) | async-done | bytes 4194320 | tf_op jit(solution)/shard_map/all_gather | solution.py:35
  46.1 11.7 %fusion.22 = f32[1024,1792]{1,0:T(8,128)S(1)} fusion(bf16[1024,2048]{1,0:T(8,128)(2,1)} %all-gather.3.cloned.1.call-done, bf16[2048,1792]{1,0:T(8,128)(2,1)} %param.7), kind=kOutput, calls=%fused_computation.37 | convolution fusion | flops 7516192768 | bytes 18874368 | tf_op jit(solution)/shard_map/dot_general | solution.py:34
  57.8 3.0 copy-done.2
  60.8 11.6 %multiply_convert_fusion.1 = bf16[1024,2048]{1,0:T(8,128)(2,1)} fusion(bf16[1,1792,2048]{2,1,0:T(8,128)(2,1)} %param.8, f32[1024,1792]{1,0:T(8,128)S(1)} %fusion.22), kind=kOutput, calls=%fused_computation.22 | convolution fusion | flops 7529562112 | bytes 18874368 | tf_op jit(solution)/shard_map/dot_general | solution.py:42
  72.5 44.7 %reduce-scatter.2.cloned.1.call-done = bf16[256,2048]{1,0:T(8,128)(2,1)} async-done(((bf16[1024,2048]{1,0:T(8,128)(2,1)}), bf16[256,2048]{1,0:T(8,128)(2,1)}) %reduce-scatter.2.cloned.1.call-update) | async-done | bytes 1048592 | tf_op jit(solution)/shard_map/reduce_scatter | solution.py:41
  117.2 2.6 subtract_convert_fusion.2
  119.9 34.5 %all-gather.5.cloned.1.call-done = bf16[1024,2048]{1,0:T(8,128)(2,1)} async-done(((bf16[256,2048]{1,0:T(8,128)(2,1)}), bf16[1024,2048]{1,0:T(8,128)(2,1)}) %all-gather.5.cloned.1.call-update) | async-done | bytes 4194320 | tf_op jit(solution)/shard_map/all_gather | solution.py:53
  154.4 14.9 %subtract_convert_fusion.1 = bf16[1792,2048]{1,0:T(8,128)(2,1)} fusion(bf16[1024,2048]{1,0:T(8,128)(2,1)} %all-gather.5.cloned.1.call-done, bf16[1,1792,2048]{2,1,0:T(8,128)(2,1)} %param.8, f32[1024,1792]{1,0:T(8,128)} %copy-done.2), kind=kOutput, calls=%fused_computation.21 | convolution fusion | flops 7540047872 | bytes 26214400 | tf_op jit(solution)/shard_map/dot_general | solution.py:51
  169.3 3.3 collective-permute-start.3
  172.7 1.4 collective-permute-start.1
  174.1 1.5 collective-permute-start.2
  175.6 0.1 dynamic-slice_convert_fusion.2
  175.7 0.6 fusion.21
  176.3 0.6 fusion.18
  176.9 0.6 fusion.20
  177.5 0.6 fusion.19
  178.1 153.4 %collective-permute-done.3 = bf16[1792,2048]{1,0:T(8,128)(2,1)} collective-permute-done((bf16[1792,2048]{1,0:T(8,128)(2,1)}, bf16[1792,2048]{1,0:T(8,128)(2,1)}, u32[]{:S(2)}, u32[]{:S(2)}) %collective-permute-start.3) | collective-permute-done | bytes 7340064 | tf_op jit(solution)/shard_map/ppermute | solution.py:12
  331.4 157.3 %collective-permute-done.1 = bf16[1792,2048]{1,0:T(8,128)(2,1)} collective-permute-done((bf16[1792,2048]{1,0:T(8,128)(2,1)}, bf16[1792,2048]{1,0:T(8,128)(2,1)}, u32[]{:S(2)}, u32[]{:S(2)}) %collective-permute-start.1) | collective-permute-done | bytes 7340064 | tf_op jit(solution)/shard_map/ppermute | solution.py:12
  488.7 157.5 %collective-permute-done.2 = bf16[1792,2048]{1,0:T(8,128)(2,1)} collective-permute-done((bf16[1792,2048]{1,0:T(8,128)(2,1)}, bf16[1792,2048]{1,0:T(8,128)(2,1)}, u32[]{:S(2)}, u32[]{:S(2)}) %collective-permute-start.2) | collective-permute-done | bytes 7340064 | tf_op jit(solution)/shard_map/ppermute | solution.py:12
  646.3 0.9 collective-permute-done
  647.1 27.4 %multiply_convert_fusion = bf16[1792,2048]{1,0:T(8,128)(2,1)} fusion(bf16[1792,2048]{1,0:T(8,128)(2,1)} %collective-permute-done.3, bf16[1792,2048]{1,0:T(8,128)(2,1)} %subtract_convert_fusion.1, bf16[1792,2048]{1,0:T(8,128)(2,1)} %collective-permute-done.1, bf16[1792,2048]{1,0:T(8,128)(2,1)} %collective-permute-done.2, ...), kind=kLoop, calls=%fused_computation.20 | loop fusion | flops 132120576 | bytes 44040240 | tf_op jit(solution)/shard_map/convert_element_type | solution.py:21
  674.5 238.3 %all-reduce.2.cloned.1.call-done = bf16[1792,2048]{1,0:T(8,128)(2,1)} async-done(((bf16[1792,2048]{1,0:T(8,128)(2,1)}), bf16[1792,2048]{1,0:T(8,128)(2,1)}) %all-reduce.2.cloned.1.call-update) | async-done | bytes 7340048 | tf_op jit(solution)/shard_map/psum | solution.py:70
  912.8 12.7 %fusion.12 = bf16[1,1792,2048]{2,1,0:T(8,128)(2,1)} fusion(bf16[1792,2048]{1,0:T(8,128)(2,1)} %all-reduce.2.cloned.1.call-done, bf16[1792,2048]{1,0:T(8,128)(2,1)} %multiply_convert_fusion), kind=kLoop, calls=%fused_computation.23 | loop fusion | flops 18350080 | bytes 22020096 | tf_op jit(solution)/shard_map/broadcast_in_dim | solution.py:72
  (14 shorter events, 0.2 us)
Async XLA Ops:
  6.5 39.6 %all-gather.3.cloned.1.call-start = ((), (), s32[]{:S(2)}) async-start(), calls=%async_computation.1 | async-start | bytes 5242880 | tf_op jit(solution)/shard_map/all_gather | solution.py:35
  7.3 109.9 %reduce-scatter.2.cloned.1.call-start = ((), (), s32[]{:S(2)}) async-start(), calls=%async_computation.2 | async-start | bytes 5242880 | tf_op jit(solution)/shard_map/reduce_scatter | solution.py:41
  57.8 3.1 copy-start.2
  60.8 56.4 %copy-start = (bf16[256,2048]{1,0:T(8,128)(2,1)S(1)}, bf16[256,2048]{1,0:T(8,128)(2,1)}, u32[]{:S(2)}) copy-start(bf16[256,2048]{1,0:T(8,128)(2,1)} %param.6) | copy-start | bytes 3145732
  72.5 82.0 %all-gather.5.cloned.1.call-start = ((), (), s32[]{:S(2)}) async-start(), calls=%async_computation.3 | async-start | bytes 5242880 | tf_op jit(solution)/shard_map/all_gather | solution.py:53
  119.8 55.8 %copy-start.1 = (s32[2,8,3]{1,0,2:T(2,128)S(1)}, s32[2,8,3]{1,0,2:T(2,128)}, u32[]{:S(2)}) copy-start(s32[2,8,3]{1,0,2:T(2,128)} %param.9) | copy-start | bytes 580
  119.8 793.0 %all-reduce.2.cloned.1.call-start = ((), (), s32[]{:S(2)}) async-start(), calls=%async_computation.4 | async-start | bytes 14680064 | tf_op jit(solution)/shard_map/psum | solution.py:70
  169.3 162.1 %collective-permute-start.3 = (bf16[1792,2048]{1,0:T(8,128)(2,1)}, bf16[1792,2048]{1,0:T(8,128)(2,1)}, u32[]{:S(2)}, u32[]{:S(2)}) collective-permute-start(bf16[1792,2048]{1,0:T(8,128)(2,1)} %subtract_convert_fusion.1), channel_id=1, source_target_pairs={{0,24},{4,28},{8,0},{12,4},{16,8},{20,12},{24,16},{28,20},{1,25},{... | collective-permute-start | bytes 22020104 | tf_op jit(solution)/shard_map/ppermute | solution.py:12
  172.7 316.1 %collective-permute-start.1 = (bf16[1792,2048]{1,0:T(8,128)(2,1)}, bf16[1792,2048]{1,0:T(8,128)(2,1)}, u32[]{:S(2)}, u32[]{:S(2)}) collective-permute-start(bf16[1792,2048]{1,0:T(8,128)(2,1)} %subtract_convert_fusion.1), channel_id=1, source_target_pairs={{0,28},{4,0},{8,4},{12,8},{16,12},{20,16},{24,20},{28,24},{1,29},{... | collective-permute-start | bytes 22020104 | tf_op jit(solution)/shard_map/ppermute | solution.py:12
  174.1 472.2 %collective-permute-start.2 = (bf16[1792,2048]{1,0:T(8,128)(2,1)}, bf16[1792,2048]{1,0:T(8,128)(2,1)}, u32[]{:S(2)}, u32[]{:S(2)}) collective-permute-start(bf16[1792,2048]{1,0:T(8,128)(2,1)} %subtract_convert_fusion.1), channel_id=1, source_target_pairs={{0,8},{4,12},{8,16},{12,20},{16,24},{20,28},{24,0},{28,4},{1,9},{5... | collective-permute-start | bytes 22020104 | tf_op jit(solution)/shard_map/ppermute | solution.py:12
  175.6 471.5 %collective-permute-start = (bf16[1792,2048]{1,0:T(8,128)(2,1)}, bf16[1792,2048]{1,0:T(8,128)(2,1)}, u32[]{:S(2)}, u32[]{:S(2)}) collective-permute-start(bf16[1792,2048]{1,0:T(8,128)(2,1)} %subtract_convert_fusion.1), channel_id=1, source_target_pairs={{0,4},{4,8},{8,12},{12,16},{16,20},{20,24},{24,28},{28,0},{1,5},{5... | collective-permute-start | bytes 22020104 | tf_op jit(solution)/shard_map/ppermute | solution.py:12
Sparse Core Ops, SparseCore 0:
  8.9 37.1 all-gather.2
  72.6 44.5 reduce-scatter.1
  119.9 34.4 all-gather.4
  674.7 238.1 all-reduce.1
where the time goes:
time: 932 us
  waiting for transfers between devices  826 us (89%)
  other arithmetic  42.8 us (5%)
  matrix products  38.2 us (4%)
  between operations  13.2 us (1%)
    ppermute x4, waiting for transfers between devices, passed_along(): lax.ppermute(x, axis, [(i, (i + by) % devices) for i in range(devices)])  469 us
    psum x1, waiting for transfers between devices, body(): lax.psum(mixed.astype(jnp.float32).astype(jnp.bfloat16), 'blk')  238 us
    reduce_scatter x1, waiting for transfers between devices, body(): lax.psum_scatter((jnp.dot(rows, weight, preferred_element_type=jnp.float3...  44.7 us
    all_gather x1, waiting for transfers between devices, body(): lax.all_gather(tokens, 'shard', axis=0, tiled=True)  38.8 us
    all_gather x1, waiting for transfers between devices, body(): lax.all_gather(resid, 'shard', axis=0, tiled=True)  34.5 us
    convert_element_type x1, other arithmetic, combine(): return (total / 4.0).astype(jnp.bfloat16)  27.4 us
  transfers between devices with their start and end apart: 8, of which 8 were waited for; matrix products, arithmetic and copies ran while one was open for 0% of the time, Pallas kernels for 0%

commit v1 on v0

--- a/solution.py
+++ b/solution.py
@@ -67,7 +67,9 @@
     first_self = combine(stepped, near_left, near_right, numer_of(mix_numer, 0, worker))
     first_right = combine(near_right, stepped, far_right, numer_of(mix_numer, 0, right_worker))
     mixed = combine(first_self, first_left, first_right, numer_of(mix_numer, 1, worker))
-    total = lax.psum(mixed.astype(jnp.float32).astype(jnp.bfloat16), "blk").astype(jnp.float32)
+    total = jnp.sum(
+        lax.all_gather(mixed.astype(jnp.float32).astype(jnp.bfloat16), "blk"), axis=0
+    ).astype(jnp.float32)
     average = total / jnp.float32(workers)
     return (mixed.astype(jnp.float32) - average).astype(jnp.bfloat16)[None]
 

time: 932 us -> 1830 us (1.96)
  waiting for transfers between devices: 826 us -> 1690 us
  other arithmetic: 42.8 us -> 65.8 us
    all_gather x0 -> x1, waiting for transfers between devices: none -> 1110 us  [body(): lax.all_gather(mixed.astype(jnp.float32).astype(jnp.bfloat16), 'blk')]
    psum x1 -> x0, waiting for transfers between devices: 238 us -> none  [body(): lax.psum(mixed.astype(jnp.float32).astype(jnp.bfloat16), 'blk')]
    reduce_sum x0 -> x1, other arithmetic: none -> 23 us  [body(): jnp.sum(lax.all_gather(mixed.astype(jnp.float32).astype(jnp.bfloat16), 'b...]
where the time goes in v1:
time: 1830 us
  waiting for transfers between devices  1690 us (92%)
  other arithmetic  65.8 us (4%)
  matrix products  38.2 us (2%)
    all_gather x1, waiting for transfers between devices, body(): lax.all_gather(mixed.astype(jnp.float32).astype(jnp.bfloat16), 'blk')  1110 us
    ppermute x4, waiting for transfers between devices, passed_along(): lax.ppermute(x, axis, [(i, (i + by) % devices) for i in range(devices)])  467 us
    reduce_scatter x1, waiting for transfers between devices, body(): lax.psum_scatter((jnp.dot(rows, weight, preferred_element_type=jnp.float3...  44.7 us
    all_gather x1, waiting for transfers between devices, body(): lax.all_gather(tokens, 'shard', axis=0, tiled=True)  38.8 us
  transfers between devices with their start and end apart: 8, of which 8 were waited for; matrix products, arithmetic and copies ran while one was open for 0% of the time, Pallas kernels for 0%

profile of v1, /device:TPU:0, one launch (start us, length us, event | category | flops | bytes accessed | tf_op | source)
XLA Modules:
  0.0 1825.6 jit_solution(17866897673565174988)
XLA Ops:
  6.5 0.7 all-gather.5.cloned.1.call-update
  7.3 38.8 %all-gather.5.cloned.1.call-done = bf16[1024,2048]{1,0:T(8,128)(2,1)} async-done(((bf16[256,2048]{1,0:T(8,128)(2,1)}), bf16[1024,2048]{1,0:T(8,128)(2,1)}) %all-gather.5.cloned.1.call-update) | async-done | bytes 4194320 | tf_op jit(solution)/shard_map/all_gather | solution.py:35
  46.1 11.7 fusion.22
  57.8 3.0 copy-done.2
  60.8 11.6 multiply_convert_fusion.1
  72.5 44.7 %reduce-scatter.2.cloned.1.call-done = bf16[256,2048]{1,0:T(8,128)(2,1)} async-done(((bf16[1024,2048]{1,0:T(8,128)(2,1)}), bf16[256,2048]{1,0:T(8,128)(2,1)}) %reduce-scatter.2.cloned.1.call-update) | async-done | bytes 1048592 | tf_op jit(solution)/shard_map/reduce_scatter | solution.py:41
  117.2 2.6 subtract_convert_fusion.2
  119.9 34.5 %all-gather.7.cloned.1.call-done = bf16[1024,2048]{1,0:T(8,128)(2,1)} async-done(((bf16[256,2048]{1,0:T(8,128)(2,1)}), bf16[1024,2048]{1,0:T(8,128)(2,1)}) %all-gather.7.cloned.1.call-update) | async-done | bytes 4194320 | tf_op jit(solution)/shard_map/all_gather | solution.py:53
  154.4 14.9 subtract_convert_fusion.1
  169.3 3.3 collective-permute-start.3
  172.7 4.7 collective-permute-start.1
  177.4 0.1 dynamic-slice_convert_fusion.2
  177.5 0.6 fusion.19
  178.1 0.6 fusion.21
  178.7 0.6 fusion.20
  179.3 0.6 fusion.18
  179.9 151.5 %collective-permute-done.3 = bf16[1792,2048]{1,0:T(8,128)(2,1)} collective-permute-done((bf16[1792,2048]{1,0:T(8,128)(2,1)}, bf16[1792,2048]{1,0:T(8,128)(2,1)}, u32[]{:S(2)}, u32[]{:S(2)}) %collective-permute-start.3) | collective-permute-done | bytes 7340064 | tf_op jit(solution)/shard_map/ppermute | solution.py:12
  331.4 158.3 %collective-permute-done.2 = bf16[1792,2048]{1,0:T(8,128)(2,1)} collective-permute-done((bf16[1792,2048]{1,0:T(8,128)(2,1)}, bf16[1792,2048]{1,0:T(8,128)(2,1)}, u32[]{:S(2)}, u32[]{:S(2)}) %collective-permute-start.2) | collective-permute-done | bytes 7340064 | tf_op jit(solution)/shard_map/ppermute | solution.py:12
  489.7 155.6 %collective-permute-done.1 = bf16[1792,2048]{1,0:T(8,128)(2,1)} collective-permute-done((bf16[1792,2048]{1,0:T(8,128)(2,1)}, bf16[1792,2048]{1,0:T(8,128)(2,1)}, u32[]{:S(2)}, u32[]{:S(2)}) %collective-permute-start.1) | collective-permute-done | bytes 7340064 | tf_op jit(solution)/shard_map/ppermute | solution.py:12
  645.3 1.8 collective-permute-done
  647.1 27.4 %multiply_convert_fusion = bf16[1792,2048]{1,0:T(8,128)(2,1)} fusion(bf16[1792,2048]{1,0:T(8,128)(2,1)} %collective-permute-done.3, bf16[1792,2048]{1,0:T(8,128)(2,1)} %subtract_convert_fusion.1, bf16[1792,2048]{1,0:T(8,128)(2,1)} %collective-permute-done.1, bf16[1792,2048]{1,0:T(8,128)(2,1)} %collective-permute-done.2, ...), kind=kLoop, calls=%fused_computation.20 | loop fusion | flops 132120576 | bytes 44040240 | tf_op jit(solution)/shard_map/convert_element_type | solution.py:21
  674.5 1108.8 %all-gather.9.cloned.1.call-done = bf16[14336,2048]{1,0:T(8,128)(2,1)} async-done(((bf16[1792,2048]{1,0:T(8,128)(2,1)}), bf16[14336,2048]{1,0:T(8,128)(2,1)}) %all-gather.9.cloned.1.call-update) | async-done | bytes 58720272 | tf_op jit(solution)/shard_map/all_gather | solution.py:71
  1783.3 23.0 %reduce_sum.12 = bf16[1792,2048]{1,0:T(8,128)(2,1)} reduce(bf16[8,1792,2048]{2,1,0:T(8,128)(2,1)} %bitcast.24, bf16[]{:T(256)} %constant.60.clone.1), dimensions={0}, to_apply=%region_1.2 | reduce | flops 25690112 | bytes 66060288 | tf_op jit(solution)/shard_map/reduce_sum | solution.py:70
  1806.4 12.7 fusion.12
  (15 shorter events, 0.2 us)
Async XLA Ops:
  6.5 39.6 %all-gather.5.cloned.1.call-start = ((), (), s32[]{:S(2)}) async-start(), calls=%async_computation.1 | async-start | bytes 5242880 | tf_op jit(solution)/shard_map/all_gather | solution.py:35
  7.3 109.9 %reduce-scatter.2.cloned.1.call-start = ((), (), s32[]{:S(2)}) async-start(), calls=%async_computation.2 | async-start | bytes 5242880 | tf_op jit(solution)/shard_map/reduce_scatter | solution.py:41
  57.8 3.1 copy-start.2
  60.8 56.4 %copy-start = (bf16[256,2048]{1,0:T(8,128)(2,1)S(1)}, bf16[256,2048]{1,0:T(8,128)(2,1)}, u32[]{:S(2)}) copy-start(bf16[256,2048]{1,0:T(8,128)(2,1)} %param.6) | copy-start | bytes 3145732
  72.5 82.0 %all-gather.7.cloned.1.call-start = ((), (), s32[]{:S(2)}) async-start(), calls=%async_computation.3 | async-start | bytes 5242880 | tf_op jit(solution)/shard_map/all_gather | solution.py:53
  119.8 57.6 %copy-start.1 = (s32[2,8,3]{1,0,2:T(2,128)S(1)}, s32[2,8,3]{1,0,2:T(2,128)}, u32[]{:S(2)}) copy-start(s32[2,8,3]{1,0,2:T(2,128)} %param.9) | copy-start | bytes 580
  119.8 1663.5 %all-gather.9.cloned.1.call-start = ((), (), s32[]{:S(2)}) async-start(), calls=%async_computation.4 | async-start | bytes 66060288 | tf_op jit(solution)/shard_map/all_gather | solution.py:71
  169.3 162.1 %collective-permute-start.3 = (bf16[1792,2048]{1,0:T(8,128)(2,1)}, bf16[1792,2048]{1,0:T(8,128)(2,1)}, u32[]{:S(2)}, u32[]{:S(2)}) collective-permute-start(bf16[1792,2048]{1,0:T(8,128)(2,1)} %subtract_convert_fusion.1), channel_id=1, source_target_pairs={{0,24},{4,28},{8,0},{12,4},{16,8},{20,12},{24,16},{28,20},{1,25},{... | collective-permute-start | bytes 22020104 | tf_op jit(solution)/shard_map/ppermute | solution.py:12
  172.7 317.0 %collective-permute-start.2 = (bf16[1792,2048]{1,0:T(8,128)(2,1)}, bf16[1792,2048]{1,0:T(8,128)(2,1)}, u32[]{:S(2)}, u32[]{:S(2)}) collective-permute-start(bf16[1792,2048]{1,0:T(8,128)(2,1)} %subtract_convert_fusion.1), channel_id=1, source_target_pairs={{0,8},{4,12},{8,16},{12,20},{16,24},{20,28},{24,0},{28,4},{1,9},{5... | collective-permute-start | bytes 22020104 | tf_op jit(solution)/shard_map/ppermute | solution.py:12
  172.7 472.6 %collective-permute-start.1 = (bf16[1792,2048]{1,0:T(8,128)(2,1)}, bf16[1792,2048]{1,0:T(8,128)(2,1)}, u32[]{:S(2)}, u32[]{:S(2)}) collective-permute-start(bf16[1792,2048]{1,0:T(8,128)(2,1)} %subtract_convert_fusion.1), channel_id=1, source_target_pairs={{0,28},{4,0},{8,4},{12,8},{16,12},{20,16},{24,20},{28,24},{1,29},{... | collective-permute-start | bytes 22020104 | tf_op jit(solution)/shard_map/ppermute | solution.py:12
  177.4 469.7 %collective-permute-start = (bf16[1792,2048]{1,0:T(8,128)(2,1)}, bf16[1792,2048]{1,0:T(8,128)(2,1)}, u32[]{:S(2)}, u32[]{:S(2)}) collective-permute-start(bf16[1792,2048]{1,0:T(8,128)(2,1)} %subtract_convert_fusion.1), channel_id=1, source_target_pairs={{0,4},{4,8},{8,12},{12,16},{16,20},{20,24},{24,28},{28,0},{1,5},{5... | collective-permute-start | bytes 22020104 | tf_op jit(solution)/shard_map/ppermute | solution.py:12
Sparse Core Ops, SparseCore 0:
  8.9 37.1 all-gather.4
  72.6 44.5 reduce-scatter.1
  119.9 34.4 all-gather.6
  674.7 1108.6 all-gather.8
